TPU v7x, 32 devices: a whole 2x2x4 slice. The times are simulated.
32 devices in a mesh: rows: 8 (over z, x), tp: 2 (over core), job: 2 (over y).
Axes of the slice: x: 2, y: 2, z: 4, core: 2. Of those that a mesh axis runs over, the one named last changes fastest.
Arguments:
- train_query: bfloat16 [4096, 2048], P(('job', 'rows'), 'tp'), parts along dimension 0, may hold values from -0.125 to 0.125
- low_query: bfloat16 [4096, 16], P(('job', 'rows')), parts along dimension 0, may hold values from -0.125 to 0.125
- high_query: bfloat16 [32, 2048], P('job', 'tp'), parts along dimension 0, may hold values from -1.5 to 1.5
- train_key: bfloat16 [4096, 512], P(('job', 'rows'), 'tp'), parts along dimension 0, may hold values from -0.125 to 0.125
- low_key: bfloat16 [4096, 16], P(('job', 'rows')), parts along dimension 0, may hold values from -0.125 to 0.125
- high_key: bfloat16 [32, 512], P('job', 'tp'), parts along dimension 0, may hold values from -1.5 to 1.5
- train_value: bfloat16 [4096, 512], P(('job', 'rows'), 'tp'), parts along dimension 0, may hold values from -0.125 to 0.125
- low_value: bfloat16 [4096, 16], P(('job', 'rows')), parts along dimension 0, may hold values from -0.125 to 0.125
- high_value: bfloat16 [32, 512], P('job', 'tp'), parts along dimension 0, may hold values from -1.5 to 1.5
- norm_train: float32 [4096], P(('job', 'rows', 'tp')), parts along dimension 0, may hold values from 0.25 to 1.75
- norm_step: float32 [4096], P(('job', 'rows', 'tp')), parts along dimension 0, may hold values from -0.3 to 0.3
Outputs:
- serve_query: bfloat16 [4096, 2048], P(('job', 'tp')), parts along dimension 0
- serve_key: bfloat16 [1024, 2048], P(('job', 'tp')), parts along dimension 0
- serve_value: bfloat16 [1024, 2048], P(('job', 'tp')), parts along dimension 0
- serve_norm: bfloat16 [4096], P('job'), parts along dimension 0
There are 2 independent parts, one for each index of `job`. A program takes and returns all parts, laid end to end along the dimension named above; each array names one. Nothing has to cross between parts.
All inputs are finite; a program needn't handle non-finite values.
Results may differ from a plain program's by a relative error of at most 0.001.
Values may be sent and summed in bfloat16 or wider, within the bound.
A program may use at most 64 MiB of HBM per device.

v0:
```python
import jax
import jax.numpy as jnp
from jax import lax
from jax.sharding import PartitionSpec as P

mix_rate = 0.5


def local(
    train_query,
    low_query,
    high_query,
    train_key,
    low_key,
    high_key,
    train_value,
    low_value,
    high_value,
    norm_train,
    norm_step,
):
    fresh_query = train_query.astype(jnp.float32) + mix_rate * jnp.dot(
        low_query, high_query, preferred_element_type=jnp.float32
    )
    fresh_key = train_key.astype(jnp.float32) + mix_rate * jnp.dot(
        low_key, high_key, preferred_element_type=jnp.float32
    )
    fresh_value = train_value.astype(jnp.float32) + mix_rate * jnp.dot(
        low_value, high_value, preferred_element_type=jnp.float32
    )
    narrow_query, narrow_key, narrow_value = (
        fresh_query.astype(jnp.bfloat16),
        fresh_key.astype(jnp.bfloat16),
        fresh_value.astype(jnp.bfloat16),
    )
    serve_query, serve_key, serve_value = (
        lax.all_gather(narrow_query, "rows", axis=0, tiled=True),
        lax.all_gather(narrow_key, "rows", axis=0, tiled=True),
        lax.all_gather(narrow_value, "rows", axis=0, tiled=True),
    )
    serve_query, serve_key, serve_value = (serve_query.T, serve_key.T, serve_value.T)
    serve_norm = lax.all_gather(
        (norm_train + norm_step).astype(jnp.bfloat16), ("rows", "tp"), axis=0, tiled=True
    )
    return (serve_query, serve_key, serve_value, serve_norm)


def solution(mesh):
    in_specs = (
        P(("job", "rows"), "tp"),
        P(("job", "rows"), None),
        P("job", "tp"),
        P(("job", "rows"), "tp"),
        P(("job", "rows"), None),
        P("job", "tp"),
        P(("job", "rows"), "tp"),
        P(("job", "rows"), None),
        P("job", "tp"),
        P(("job", "rows", "tp")),
        P(("job", "rows", "tp")),
    )
    out_specs = (P(("job", "tp"), None), P(("job", "tp"), None), P(("job", "tp"), None), P("job"))
    return jax.shard_map(local, mesh=mesh, in_specs=in_specs, out_specs=out_specs, check_vma=False)
```

profile of v0, /device:TPU:0, one launch (start us, length us, event | category | flops | bytes accessed | tf_op | source)
XLA Modules:
  0.0 182.1 jit_solution(1494663022165520071)
XLA Ops:
  7.2 0.0 copy-start
  7.2 0.0 all-gather.7.cloned.1.call-start
  7.2 1.8 %fusion.4 = bf16[256,256]{1,0:T(8,128)(2,1)} fusion(bf16[256,16]{0,1:T(8,128)(2,1)} %param.15, bf16[16,256]{1,0:T(8,128)(2,1)} %param.16, bf16[256,256]{1,0:T(8,128)(2,1)} %param.14), kind=kOutput, calls=%fused_computation.7 | convolution fusion | flops 2359296 | bytes 278528 | tf_op jit(solution)/shard_map/dot_general | solution.py:25
  9.1 0.0 all-gather.7.cloned.1.call-update
  9.1 0.0 all-gather.9.cloned.1.call-start
  9.1 1.8 fusion.5
  10.9 0.0 all-gather.9.cloned.1.call-update
  11.0 0.0 all-gather.5.cloned.1.call-start
  11.0 0.0 copy-done
  11.0 2.2 %fusion.1 = bf16[256,1024]{1,0:T(8,128)(2,1)} fusion(bf16[256,16]{0,1:T(8,128)(2,1)} %param.12, bf16[16,1024]{1,0:T(8,128)(2,1)S(1)} %copy-done, bf16[256,1024]{1,0:T(8,128)(2,1)} %param.11), kind=kOutput, calls=%fused_computation.2 | convolution fusion | flops 9437184 | bytes 1089536 | tf_op jit(solution)/shard_map/dot_general | solution.py:22
  13.2 0.0 all-gather.5.cloned.1.call-update
  13.2 0.7 convert_bitcast_fusion
  13.9 23.1 %all-gather = bf16[16,1,128]{2,1,0:T(2,128)(2,1)S(1)} all-gather(bf16[1,1,128]{2,1,0:T(2,128)(2,1)S(1)} %convert_bitcast_fusion), channel_id=1, replica_groups=mesh['rows'=8,'tp'=2,'job'=2] {'rows','tp'}, dimensions={0}, use_global_device_ids=true | all-gather | bytes 4352 | tf_op jit(solution)/shard_map/all_gather | solution.py:42
  37.0 0.6 reduce
  37.6 16.1 %all-gather.7.cloned.1.call-done = bf16[2048,256]{1,0:T(8,128)(2,1)} async-done(((bf16[256,256]{1,0:T(8,128)(2,1)}), bf16[2048,256]{1,0:T(8,128)(2,1)}) %all-gather.7.cloned.1.call-update) | async-done | bytes 1048592 | tf_op jit(solution)/shard_map/all_gather | solution.py:38
  53.7 2.3 %copy.22 = bf16[256,2048]{1,0:T(8,128)(2,1)} copy(bf16[256,2048]{0,1:T(8,128)(2,1)} %bitcast.13) | data formatting | bytes 2097152
  56.0 38.9 %all-gather.9.cloned.1.call-done = bf16[2048,256]{1,0:T(8,128)(2,1)} async-done(((bf16[256,256]{1,0:T(8,128)(2,1)}), bf16[2048,256]{1,0:T(8,128)(2,1)}) %all-gather.9.cloned.1.call-update) | async-done | bytes 1048592 | tf_op jit(solution)/shard_map/all_gather | solution.py:39
  94.9 2.3 %copy.23 = bf16[256,2048]{1,0:T(8,128)(2,1)} copy(bf16[256,2048]{0,1:T(8,128)(2,1)} %bitcast.14) | data formatting | bytes 2097152
  97.1 72.0 %all-gather.5.cloned.1.call-done = bf16[2048,1024]{1,0:T(8,128)(2,1)} async-done(((bf16[256,1024]{1,0:T(8,128)(2,1)}), bf16[2048,1024]{1,0:T(8,128)(2,1)}) %all-gather.5.cloned.1.call-update) | async-done | bytes 4194320 | tf_op jit(solution)/shard_map/all_gather | solution.py:37
  169.1 6.4 %copy.21 = bf16[1024,2048]{1,0:T(8,128)(2,1)} copy(bf16[1024,2048]{0,1:T(8,128)(2,1)} %bitcast.12) | data formatting | bytes 8388608
Async XLA Ops:
  7.2 3.9 %copy-start = (bf16[16,1024]{1,0:T(8,128)(2,1)S(1)}, bf16[16,1024]{1,0:T(8,128)(2,1)}, u32[]{:S(2)}) copy-start(bf16[16,1024]{1,0:T(8,128)(2,1)} %param.13) | copy-start | bytes 98308
  7.2 46.5 %all-gather.7.cloned.1.call-start = ((), (), s32[]{:S(2)}) async-start(), calls=%async_computation.1 | async-start | bytes 1179648 | tf_op jit(solution)/shard_map/all_gather | solution.py:38
  9.1 85.8 %all-gather.9.cloned.1.call-start = ((), (), s32[]{:S(2)}) async-start(), calls=%async_computation.2 | async-start | bytes 1179648 | tf_op jit(solution)/shard_map/all_gather | solution.py:39
  11.0 158.1 %all-gather.5.cloned.1.call-start = ((), (), s32[]{:S(2)}) async-start(), calls=%async_computation | async-start | bytes 4718592 | tf_op jit(solution)/shard_map/all_gather | solution.py:37
Sparse Core Ops, SparseCore 0:
  10.7 42.9 all-gather.6
  55.8 38.9 all-gather.8
  97.6 71.4 all-gather.4
where the time goes:
time: 182 us
  waiting for transfers between devices  127 us (70%)
  blocking collectives  23.1 us (13%)
  between operations  13.8 us (8%)
  local copies, waits for them, and re-layouts  11 us (6%)
  matrix products  5.81 us (3%)
    all_gather x1, waiting for transfers between devices, local(): lax.all_gather(narrow_query, 'rows', axis=0, tiled=True)  72 us
    all_gather x1, waiting for transfers between devices, local(): lax.all_gather(narrow_value, 'rows', axis=0, tiled=True)  38.9 us
    all_gather x1, blocking collectives, local(): lax.all_gather((norm_train + norm_step).astype(jnp.bfloat16), ('rows', 't...  23.1 us
    all_gather x1, waiting for transfers between devices, local(): lax.all_gather(narrow_key, 'rows', axis=0, tiled=True)  16.1 us
    unnamed x5, local copies, waits for them, and re-layouts  11 us
  transfers between devices with their start and end apart: 3, of which 3 were waited for; matrix products, arithmetic and copies ran while one was open for 5% of the time, Pallas kernels for 0%

commit v1 on v0

v1 whole, which is shorter than its diff:
```python
import functools

import jax
import jax.numpy as jnp
from jax import lax
from jax.experimental import pallas as pl
from jax.experimental.pallas import tpu as pltpu
from jax.sharding import PartitionSpec as P

mix_rate = 0.5
CHUNK_ROWS = 128
MESH = pl.DeviceIdType.MESH


def kernel(
    size,
    tp_size,
    *refs,
):
    given, refs = refs[:11], refs[11:]
    serve_query, serve_key, serve_value, serve_norm = refs[:4]
    held, refs = refs[4:15], refs[15:]
    run_kernel(size, tp_size, given, held, serve_query, serve_key, serve_value, serve_norm, *refs)


def run_kernel(
    size,
    tp_size,
    given,
    held,
    serve_query,
    serve_key,
    serve_value,
    serve_norm,
    gains,
    load_sem,
    send_sem,
    recv_sem,
    gain_send,
    gain_recv,
):
    loads = [
        pltpu.make_async_copy(g, h, load_sem.at[n]) for n, (g, h) in enumerate(zip(given, held))
    ]
    for load in loads:
        load.start()
    (
        train_query,
        low_query,
        high_query,
        train_key,
        low_key,
        high_key,
        train_value,
        low_value,
        high_value,
        norm_train,
        norm_step,
    ) = held
    depth = size // 2
    me = lax.axis_index("rows")
    core = lax.axis_index("tp")
    z, x = me // 2, lax.rem(me, 2)
    other = 1 - x
    width = train_query.shape[0]
    up, down, side = me + 2, me - 2, 2 * z + other
    targets = (up, down, side)
    has_up, has_down = z < depth - 1, z > 0
    UP, DOWN, SIDE = 0, 1, 2

    seats = size * tp_size
    seat = me * tp_size + core

    def peer(k):
        p = lax.rem(seat + k, seats)
        return {"rows": p // tp_size, "tp": lax.rem(p, tp_size)}

    barrier = pltpu.get_barrier_semaphore()
    for k in range(1, seats):
        pl.semaphore_signal(barrier, inc=1, device_id=peer(k), device_id_type=MESH)

    chunks = []
    for train, low, high, serve in (
        (train_query, low_query, high_query, serve_query),
        (train_key, low_key, high_key, serve_key),
        (train_value, low_value, high_value, serve_value),
    ):
        for start in range(0, serve.shape[0], CHUNK_ROWS):
            chunks.append((train, low, high, serve, start))
    count = len(chunks)

    def piece(item, c):
        serve, start = chunks[c][3], chunks[c][4]
        return serve.at[
            pl.ds(start, CHUNK_ROWS), pl.ds(pl.multiple_of(item * width, 128), width)
        ]

    def copy(item, c, way):
        ref = piece(item, c)
        return pltpu.make_async_remote_copy(
            src_ref=ref,
            dst_ref=ref,
            send_sem=send_sem.at[way, item, c],
            recv_sem=recv_sem.at[item, c],
            device_id={"rows": targets[way]},
            device_id_type=MESH,
        )

    def arrive(item, c):
        copy(item, c, SIDE).wait_recv()

    def crossing(c):
        return c % 2 == 1

    def merge(c):
        train, low, high, serve, start = chunks[c]
        rows = pl.ds(start, CHUNK_ROWS)
        update = lax.dot_general(
            high[:, rows], low[...], (((0,), (0,)), ((), ())), preferred_element_type=jnp.float32
        )
        fresh = train[:, rows].T.astype(jnp.float32) + mix_rate * update
        serve[rows, pl.ds(pl.multiple_of(me * width, 128), width)] = fresh.astype(jnp.bfloat16)

    def send_own(c):
        @pl.when(has_down)
        def _():
            copy(me, c, DOWN).start()

        @pl.when(has_up)
        def _():
            copy(me, c, UP).start()

        copy(me, c, SIDE).start()

    def gain_copy(k):
        return pltpu.make_async_remote_copy(
            src_ref=gains.at[seat],
            dst_ref=gains.at[seat],
            send_sem=gain_send.at[k],
            recv_sem=gain_recv.at[k],
            device_id=peer(k),
            device_id_type=MESH,
        )

    for load in loads:
        load.wait()
    gains[pl.ds(seat, 1)] = (norm_train[...] + norm_step[...])[None]
    merge(0)
    merge(1)
    pl.semaphore_wait(barrier, seats - 1)
    for c in range(2, count + 2):
        send_own(c - 2)
        if c < count:
            merge(c)
    for k in range(1, seats):
        gain_copy(k).start()

    def pass_on(step, c):
        below, above = me - 2 * step, me + 2 * step

        @pl.when(z >= step)
        def _():
            arrive(below, c)

            @pl.when(has_up)
            def _():
                copy(below, c, UP).start()

            if not (step == 1 and crossing(c)):
                copy(below, c, SIDE).start()

        @pl.when(z + step < depth)
        def _():
            arrive(above, c)

            @pl.when(has_down)
            def _():
                copy(above, c, DOWN).start()

            if not (step == 1 and crossing(c)):
                copy(above, c, SIDE).start()

    def cross(c):
        arrive(side, c)

        @pl.when(has_down)
        def _():
            copy(side, c, DOWN).start()

        @pl.when(has_up)
        def _():
            copy(side, c, UP).start()

    for step in range(1, depth):
        for c in range(count):
            pass_on(step, c)
        if step == max(1, depth - 2):
            for c in range(count):
                if crossing(c):
                    cross(c)

    for c in range(count):
        if not crossing(c):
            arrive(side, c)
    for step in range(1, depth):
        for c in range(count):
            @pl.when(z >= step)
            def _():
                arrive(side - 2 * step, c)

            @pl.when(z + step < depth)
            def _():
                arrive(side + 2 * step, c)

    for k in range(1, seats):
        gain_copy(k).wait_recv()
    serve_norm[...] = gains[...].reshape(serve_norm.shape).astype(jnp.bfloat16)

    for k in range(1, seats):
        gain_copy(k).wait_send()
    for c in range(count):
        copy(me, c, SIDE).wait_send()

        @pl.when(has_down)
        def _():
            copy(me, c, DOWN).wait_send()
            if crossing(c):
                copy(side, c, DOWN).wait_send()

        @pl.when(has_up)
        def _():
            copy(me, c, UP).wait_send()
            if crossing(c):
                copy(side, c, UP).wait_send()

        for step in range(1, depth):
            below, above = me - 2 * step, me + 2 * step

            @pl.when(z >= step)
            def _():
                @pl.when(has_up)
                def _():
                    copy(below, c, UP).wait_send()

                if not (step == 1 and crossing(c)):
                    copy(below, c, SIDE).wait_send()

            @pl.when(z + step < depth)
            def _():
                @pl.when(has_down)
                def _():
                    copy(above, c, DOWN).wait_send()

                if not (step == 1 and crossing(c)):
                    copy(above, c, SIDE).wait_send()


def fused(size, tp_size, *args):
    train_query, train_key, train_value, norm_train = args[0], args[3], args[6], args[9]
    seats, norm_length = size * tp_size, norm_train.shape[0]
    args = [a.T if n in (1, 4, 7) else a for n, a in enumerate(args)]
    args = [a.reshape(1, -1) if a.ndim == 1 else a for a in args]
    full = train_query.shape[0] * size
    outs = [
        pltpu.VMEM((t.shape[1], full), jnp.bfloat16)
        for t in (train_query, train_key, train_value)
    ]
    outs.append(pltpu.VMEM((seats, norm_length), jnp.bfloat16))
    count = sum(t.shape[1] for t in (train_query, train_key, train_value)) // CHUNK_ROWS
    vmem = pl.BlockSpec(memory_space=pltpu.VMEM)
    query, key, value, norm = pl.pallas_call(
        functools.partial(kernel, size, tp_size),
        out_shape=outs,
        in_specs=[pl.BlockSpec(memory_space=pltpu.HBM)] * 11,
        out_specs=[vmem] * 4,
        scratch_shapes=[pltpu.VMEM(a.shape, a.dtype) for a in args]
        + [
            pltpu.VMEM((seats, 1, norm_length), jnp.float32),
            pltpu.SemaphoreType.DMA((11,)),
            pltpu.SemaphoreType.DMA((3, size, count)),
            pltpu.SemaphoreType.DMA((size, count)),
            pltpu.SemaphoreType.DMA((seats,)),
            pltpu.SemaphoreType.DMA((seats,)),
        ],
        compiler_params=pltpu.CompilerParams(
            collective_id=0, has_side_effects=True, vmem_limit_bytes=16 * 2**20
        ),
    )(*args)
    query, key, value, norm = store_out(query, key, value, norm)
    return query, key, value, norm.reshape(-1)


def store_kernel(*refs):
    ins, outs, sems = refs[:4], refs[4:8], refs[8]
    copies = [pltpu.make_async_copy(i, o, sems.at[n]) for n, (i, o) in enumerate(zip(ins, outs))]
    for c in copies:
        c.start()
    for c in copies:
        c.wait()


def store_out(*arrays):
    return pl.pallas_call(
        store_kernel,
        out_shape=[jax.ShapeDtypeStruct(a.shape, a.dtype) for a in arrays],
        in_specs=[pl.BlockSpec(memory_space=pltpu.VMEM)] * 4,
        out_specs=[pl.BlockSpec(memory_space=pltpu.HBM)] * 4,
        scratch_shapes=[pltpu.SemaphoreType.DMA((4,))],
        compiler_params=pltpu.CompilerParams(vmem_limit_bytes=16 * 2**20),
    )(*arrays)


def plain(
    train_query,
    low_query,
    high_query,
    train_key,
    low_key,
    high_key,
    train_value,
    low_value,
    high_value,
    norm_train,
    norm_step,
):
    def merged(train, low, high):
        update = jnp.dot(low, high, preferred_element_type=jnp.float32)
        fresh = train.astype(jnp.float32) + mix_rate * update
        return lax.all_gather(fresh.astype(jnp.bfloat16), "rows", axis=0, tiled=True).T

    serve_norm = lax.all_gather(
        (norm_train + norm_step).astype(jnp.bfloat16), ("rows", "tp"), axis=0, tiled=True
    )
    return (
        merged(train_query, low_query, high_query),
        merged(train_key, low_key, high_key),
        merged(train_value, low_value, high_value),
        serve_norm,
    )


def solution(mesh):
    size, tp_size = mesh.shape["rows"], mesh.shape["tp"]

    def local(*args):
        trains = (args[0], args[3], args[6])
        fits = (
            size % 2 == 0
            and size >= 4
            and all(t.shape[0] % 128 == 0 and t.shape[1] % CHUNK_ROWS == 0 for t in trains)
            and args[9].shape[0] % 128 == 0
        )
        return fused(size, tp_size, *args) if fits else plain(*args)

    in_specs = (
        P(("job", "rows"), "tp"),
        P(("job", "rows"), None),
        P("job", "tp"),
        P(("job", "rows"), "tp"),
        P(("job", "rows"), None),
        P("job", "tp"),
        P(("job", "rows"), "tp"),
        P(("job", "rows"), None),
        P("job", "tp"),
        P(("job", "rows", "tp")),
        P(("job", "rows", "tp")),
    )
    out_specs = (P(("job", "tp"), None), P(("job", "tp"), None), P(("job", "tp"), None), P("job"))
    return jax.shard_map(local, mesh=mesh, in_specs=in_specs, out_specs=out_specs, check_vma=False)
```

time: 182 us -> 83.6 us (0.46)
  waiting for transfers between devices: 127 us -> 0 us
  Pallas kernels: 0 us -> 74.1 us
  blocking collectives: 23.1 us -> 0 us
  between operations: 13.8 us -> 0.66 us
  matrix products: 5.81 us -> 0 us
  local copies, waits for them, and re-layouts: 11 us -> 8.39 us
    all_gather x3 -> x0, waiting for transfers between devices: 127 us -> none  [the longest x1 72 us: local(): lax.all_gather(narrow_query, 'rows', axis=0, tiled=True)]
    pallas_call x0 -> x2, Pallas kernels: none -> 74.1 us  [the longest x1 71.4 us: fused(): pl.pallas_call(functools.partial(kernel, size, tp_size), out_shape=outs,...]
    all_gather x1 -> x0, blocking collectives: 23.1 us -> none  [local(): lax.all_gather((norm_train + norm_step).astype(jnp.bfloat16), ('rows', 't...]
    dot_general x3 -> x0, matrix products: 5.81 us -> none  [the longest x1 2.17 us: local(): jnp.dot(low_query, high_query, preferred_element_type=jnp.float32)]
    unnamed x5 -> x22, local copies, waits for them, and re-layouts: 11 us -> 8.39 us
  transfers between devices with their start and end apart: 3 -> 0, of which waited for: 3 -> 0; matrix products, arithmetic and copies ran while one was open for 5% -> 0% of each run, Pallas kernels for 0% -> 0%
where the time goes in v1:
time: 83.6 us; the launch traced here: 83.1 us
  Pallas kernels  74.1 us (89%)
  local copies, waits for them, and re-layouts  8.39 us (10%)
    pallas_call x1, Pallas kernels, fused(): pl.pallas_call(functools.partial(kernel, size, tp_size), out_shape=outs,...  71.4 us
    unnamed x22, local copies, waits for them, and re-layouts  8.39 us
    pallas_call x1, Pallas kernels, store_out(): pl.pallas_call(store_kernel, out_shape=[jax.ShapeDtypeStruct(a.shape, a.d...  2.71 us

profile of v1, /device:TPU:0, one launch (start us, length us, event | category | flops | bytes accessed | tf_op | source)
XLA Modules:
  0.0 83.1 jit_solution(7228173134974949456)
XLA Ops:
  0.6 0.0 copy-start
  0.6 1.0 %copy-done = bf16[256,1024]{1,0:T(8,128)(2,1)S(1)} copy-done((bf16[256,1024]{1,0:T(8,128)(2,1)S(1)}, bf16[256,1024]{1,0:T(8,128)(2,1)}, u32[]{:S(2)}) %copy-start) | copy-done | bytes 524312
  1.7 0.0 copy-start.1
  1.7 0.9 %copy-done.1 = bf16[256,256]{1,0:T(8,128)(2,1)S(1)} copy-done((bf16[256,256]{1,0:T(8,128)(2,1)S(1)}, bf16[256,256]{1,0:T(8,128)(2,1)}, u32[]{:S(2)}) %copy-start.1) | copy-done | bytes 131096
  2.6 0.0 copy-start.2
  2.6 0.9 %copy-done.2 = bf16[256,256]{1,0:T(8,128)(2,1)S(1)} copy-done((bf16[256,256]{1,0:T(8,128)(2,1)S(1)}, bf16[256,256]{1,0:T(8,128)(2,1)}, u32[]{:S(2)}) %copy-start.2) | copy-done | bytes 131096
  3.5 0.0 copy-start.3
  3.5 0.8 copy-done.3
  4.2 0.0 copy-start.4
  4.2 0.7 copy-done.4
  4.9 0.0 copy-start.5
  4.9 0.7 copy-done.5
  5.6 0.0 copy-start.6
  5.6 0.7 copy-done.6
  6.3 0.0 copy-start.7
  6.3 0.7 copy-done.7
  7.0 0.0 copy-start.8
  7.0 0.7 copy-done.8
  7.7 0.0 copy-start.9
  7.7 0.7 copy-done.9
  8.4 0.0 copy-start.10
  8.4 0.7 copy-done.10
  9.0 71.4 %shard_map.138 = (bf16[1024,2048]{1,0:T(8,128)(2,1)S(1)}, bf16[256,2048]{1,0:T(8,128)(2,1)S(1)}, bf16[256,2048]{1,0:T(8,128)(2,1)S(1)}, bf16[16,128]{1,0:T(8,128)(2,1)S(1)}) custom-call(bf16[256,1024]{1,0:T(8,128)(2,1)S(1)} %copy-done, bf16[16,256]{1,0:T(8,128)(2,1)S(1)} %bitcast.6, bf16[16,1024]{1,0:T(8,128)(2,1)S(1)} %copy-done.3, ...), custom_call_target="tpu_custom_call" | custom-call | tf_op jit(solution)/shard_map/pallas_call | solution.py:271
  80.4 2.7 %shard_map.139 = (bf16[1024,2048]{1,0:T(8,128)(2,1)}, bf16[256,2048]{1,0:T(8,128)(2,1)}, bf16[256,2048]{1,0:T(8,128)(2,1)}, bf16[16,128]{1,0:T(8,128)(2,1)}) custom-call(bf16[1024,2048]{1,0:T(8,128)(2,1)S(1)} %get-tuple-element.12.refs_0_, bf16[256,2048]{1,0:T(8,128)(2,1)S(1)} %get-tuple-element.13.refs_1_, bf16[256,2048]{1,0:T(8,128)(2,1)S(1)} %get-tuple-element.14.refs_2_, ...), custom_call_target="tpu_custom_call" | custom-call | tf_op jit(solution)/shard_map/pallas_call | solution.py:303
Async XLA Ops:
  0.6 1.0 %copy-start = (bf16[256,1024]{1,0:T(8,128)(2,1)S(1)}, bf16[256,1024]{1,0:T(8,128)(2,1)}, u32[]{:S(2)}) copy-start(bf16[256,1024]{1,0:T(8,128)(2,1)} %refs_0_.1) | copy-start | bytes 1572868
  1.7 0.9 %copy-start.1 = (bf16[256,256]{1,0:T(8,128)(2,1)S(1)}, bf16[256,256]{1,0:T(8,128)(2,1)}, u32[]{:S(2)}) copy-start(bf16[256,256]{1,0:T(8,128)(2,1)} %refs_3_.1) | copy-start | bytes 393220
  2.6 0.9 %copy-start.2 = (bf16[256,256]{1,0:T(8,128)(2,1)S(1)}, bf16[256,256]{1,0:T(8,128)(2,1)}, u32[]{:S(2)}) copy-start(bf16[256,256]{1,0:T(8,128)(2,1)} %refs_6_.1) | copy-start | bytes 393220
  3.5 0.8 copy-start.3
  4.2 0.7 copy-start.4
  4.9 0.7 copy-start.5
  5.6 0.7 copy-start.6
  6.3 0.7 copy-start.7
  7.0 0.7 copy-start.8
  7.7 0.7 copy-start.9
  8.4 0.7 copy-start.10

commit v2 on v1

--- a/solution.py
+++ b/solution.py
@@ -8,7 +8,8 @@
 from jax.sharding import PartitionSpec as P
 
 mix_rate = 0.5
-CHUNK_ROWS = 128
+CHUNK_ROWS = 256
+VMEM_BYTES = 67043328
 MESH = pl.DeviceIdType.MESH
 
 
@@ -267,6 +268,8 @@
     ]
     outs.append(pltpu.VMEM((seats, norm_length), jnp.bfloat16))
     count = sum(t.shape[1] for t in (train_query, train_key, train_value)) // CHUNK_ROWS
+    grant = VMEM_BYTES - 2 * (sum(t.shape[1] for t in (train_query, train_key, train_value)) * full)
+    grant -= 2 * seats * norm_length
     vmem = pl.BlockSpec(memory_space=pltpu.VMEM)
     query, key, value, norm = pl.pallas_call(
         functools.partial(kernel, size, tp_size),
@@ -283,7 +286,7 @@
             pltpu.SemaphoreType.DMA((seats,)),
         ],
         compiler_params=pltpu.CompilerParams(
-            collective_id=0, has_side_effects=True, vmem_limit_bytes=16 * 2**20
+            collective_id=0, has_side_effects=True, vmem_limit_bytes=grant
         ),
     )(*args)
     query, key, value, norm = store_out(query, key, value, norm)

time: 83.6 us -> 72.6 us (0.87)
  local copies, waits for them, and re-layouts: 8.39 us -> 0 us
  Pallas kernels: 74.1 us -> 71.8 us
    unnamed x22 -> x0, local copies, waits for them, and re-layouts: 8.39 us -> none
    pallas_call x1, Pallas kernels: 71.4 us -> 69.1 us  [fused(): pl.pallas_call(functools.partial(kernel, size, tp_size), out_shape=outs,...]
where the time goes in v2:
time: 72.6 us; the launch traced here: 72.4 us
  Pallas kernels  71.8 us (99%)
    pallas_call x1, Pallas kernels, fused(): pl.pallas_call(functools.partial(kernel, size, tp_size), out_shape=outs,...  69.1 us
    pallas_call x1, Pallas kernels, store_out(): pl.pallas_call(store_kernel, out_shape=[jax.ShapeDtypeStruct(a.shape, a.d...  2.71 us

profile of v2, /device:TPU:0, one launch (start us, length us, event | category | flops | bytes accessed | tf_op | source)
XLA Modules:
  0.0 72.4 jit_solution(11557843018745703652)
XLA Ops:
  0.6 69.1 %shard_map.138 = (bf16[1024,2048]{1,0:T(8,128)(2,1)S(1)}, bf16[256,2048]{1,0:T(8,128)(2,1)S(1)}, bf16[256,2048]{1,0:T(8,128)(2,1)S(1)}, bf16[16,128]{1,0:T(8,128)(2,1)S(1)}) custom-call(bf16[256,1024]{1,0:T(8,128)(2,1)} %refs_0_.1, bf16[16,256]{1,0:T(8,128)(2,1)} %bitcast.6, bf16[16,1024]{1,0:T(8,128)(2,1)} %refs_2_.1, bf16[256,256]{1,0:T(8,128)(2,1)} %refs_3_.1, ...), custom_call_target="tpu_custom_call" | custom-call | tf_op jit(solution)/shard_map/pallas_call | solution.py:274
  69.7 2.7 %shard_map.139 = (bf16[1024,2048]{1,0:T(8,128)(2,1)}, bf16[256,2048]{1,0:T(8,128)(2,1)}, bf16[256,2048]{1,0:T(8,128)(2,1)}, bf16[16,128]{1,0:T(8,128)(2,1)}) custom-call(bf16[1024,2048]{1,0:T(8,128)(2,1)S(1)} %get-tuple-element.12.refs_0_, bf16[256,2048]{1,0:T(8,128)(2,1)S(1)} %get-tuple-element.13.refs_1_, bf16[256,2048]{1,0:T(8,128)(2,1)S(1)} %get-tuple-element.14.refs_2_, ...), custom_call_target="tpu_custom_call" | custom-call | tf_op jit(solution)/shard_map/pallas_call | solution.py:306

commit v3 on v2

--- a/solution.py
+++ b/solution.py
@@ -9,8 +9,24 @@
 
 mix_rate = 0.5
 CHUNK_ROWS = 256
+FIRST_ROWS = 256
 VMEM_BYTES = 67043328
 MESH = pl.DeviceIdType.MESH
+
+
+def cuts(length, first):
+    sizes = []
+    while first and length > FIRST_ROWS and length % (2 * FIRST_ROWS) == 0:
+        sizes.insert(0, min(length // 2, CHUNK_ROWS))
+        length -= sizes[0]
+    while length:
+        sizes.insert(0, min(length, FIRST_ROWS if first else CHUNK_ROWS))
+        length -= sizes[0]
+    start, found = 0, []
+    for rows in sizes:
+        found.append((start, rows))
+        start += rows
+    return found
 
 
 def kernel(
@@ -43,8 +59,6 @@
     loads = [
         pltpu.make_async_copy(g, h, load_sem.at[n]) for n, (g, h) in enumerate(zip(given, held))
     ]
-    for load in loads:
-        load.start()
     (
         train_query,
         low_query,
@@ -69,16 +83,27 @@
     has_up, has_down = z < depth - 1, z > 0
     UP, DOWN, SIDE = 0, 1, 2
 
-    seats = size * tp_size
-    seat = me * tp_size + core
-
-    def peer(k):
-        p = lax.rem(seat + k, seats)
-        return {"rows": p // tp_size, "tp": lax.rem(p, tp_size)}
+    def partner(k):
+        return {"tp": lax.rem(core + k, tp_size)}
 
     barrier = pltpu.get_barrier_semaphore()
-    for k in range(1, seats):
-        pl.semaphore_signal(barrier, inc=1, device_id=peer(k), device_id_type=MESH)
+
+    def greet(device):
+        pl.semaphore_signal(barrier, inc=1, device_id=device, device_id_type=MESH)
+
+    @pl.when(has_up)
+    def _():
+        greet({"rows": up})
+
+    @pl.when(has_down)
+    def _():
+        greet({"rows": down})
+
+    greet({"rows": side})
+    for k in range(1, tp_size):
+        greet(partner(k))
+    for load in loads:
+        load.start()
 
     chunks = []
     for train, low, high, serve in (
@@ -86,15 +111,21 @@
         (train_key, low_key, high_key, serve_key),
         (train_value, low_value, high_value, serve_value),
     ):
-        for start in range(0, serve.shape[0], CHUNK_ROWS):
-            chunks.append((train, low, high, serve, start))
+        for start, rows in cuts(serve.shape[0], not chunks):
+            chunks.append((train, low, high, serve, start, rows))
     count = len(chunks)
+    queries = sum(c[3] is serve_query for c in chunks)
+    twice, left = set(), sum(c[5] for c in chunks) // 2
+    for c in sorted(range(count), key=lambda c: -chunks[c][5]):
+        if chunks[c][5] <= left:
+            twice.add(c)
+            left -= chunks[c][5]
 
     def piece(item, c):
-        serve, start = chunks[c][3], chunks[c][4]
-        return serve.at[
-            pl.ds(start, CHUNK_ROWS), pl.ds(pl.multiple_of(item * width, 128), width)
-        ]
+        if c == count:
+            return gains.at[item]
+        serve, start, rows = chunks[c][3:]
+        return serve.at[pl.ds(start, rows), pl.ds(pl.multiple_of(item * width, 128), width)]
 
     def copy(item, c, way):
         ref = piece(item, c)
@@ -111,11 +142,11 @@
         copy(item, c, SIDE).wait_recv()
 
     def crossing(c):
-        return c % 2 == 1
+        return c in twice
 
     def merge(c):
-        train, low, high, serve, start = chunks[c]
-        rows = pl.ds(start, CHUNK_ROWS)
+        train, low, high, serve, start, length = chunks[c]
+        rows = pl.ds(start, length)
         update = lax.dot_general(
             high[:, rows], low[...], (((0,), (0,)), ((), ())), preferred_element_type=jnp.float32
         )
@@ -135,26 +166,33 @@
 
     def gain_copy(k):
         return pltpu.make_async_remote_copy(
-            src_ref=gains.at[seat],
-            dst_ref=gains.at[seat],
+            src_ref=gains.at[me, core],
+            dst_ref=gains.at[me, core],
             send_sem=gain_send.at[k],
             recv_sem=gain_recv.at[k],
-            device_id=peer(k),
+            device_id=partner(k),
             device_id_type=MESH,
         )
 
-    for load in loads:
-        load.wait()
-    gains[pl.ds(seat, 1)] = (norm_train[...] + norm_step[...])[None]
+    for n in (0, 1, 2, 9, 10):
+        loads[n].wait()
+    gains[pl.ds(me, 1), pl.ds(core, 1)] = (norm_train[...] + norm_step[...])[None, None]
     merge(0)
     merge(1)
-    pl.semaphore_wait(barrier, seats - 1)
+    pl.semaphore_wait(barrier, tp_size + has_up.astype(jnp.int32) + has_down.astype(jnp.int32))
     for c in range(2, count + 2):
         send_own(c - 2)
         if c < count:
+            if c == queries:
+                for n in range(3, 9):
+                    loads[n].wait()
             merge(c)
-    for k in range(1, seats):
-        gain_copy(k).start()
+        if c == 3:
+            for k in range(1, tp_size):
+                gain_copy(k).start()
+    for k in range(1, tp_size):
+        gain_copy(k).wait_recv()
+    send_own(count)
 
     def pass_on(step, c):
         below, above = me - 2 * step, me + 2 * step
@@ -193,18 +231,18 @@
             copy(side, c, UP).start()
 
     for step in range(1, depth):
-        for c in range(count):
+        for c in range(count + 1):
             pass_on(step, c)
         if step == max(1, depth - 2):
             for c in range(count):
                 if crossing(c):
                     cross(c)
 
-    for c in range(count):
+    for c in range(count + 1):
         if not crossing(c):
             arrive(side, c)
     for step in range(1, depth):
-        for c in range(count):
+        for c in range(count + 1):
             @pl.when(z >= step)
             def _():
                 arrive(side - 2 * step, c)
@@ -213,13 +251,11 @@
             def _():
                 arrive(side + 2 * step, c)
 
-    for k in range(1, seats):
-        gain_copy(k).wait_recv()
     serve_norm[...] = gains[...].reshape(serve_norm.shape).astype(jnp.bfloat16)
 
-    for k in range(1, seats):
+    for k in range(1, tp_size):
         gain_copy(k).wait_send()
-    for c in range(count):
+    for c in range(count + 1):
         copy(me, c, SIDE).wait_send()
 
         @pl.when(has_down)
@@ -267,7 +303,8 @@
         for t in (train_query, train_key, train_value)
     ]
     outs.append(pltpu.VMEM((seats, norm_length), jnp.bfloat16))
-    count = sum(t.shape[1] for t in (train_query, train_key, train_value)) // CHUNK_ROWS
+    lengths = [t.shape[1] for t in (train_query, train_key, train_value)]
+    count = sum(len(cuts(length, n == 0)) for n, length in enumerate(lengths))
     grant = VMEM_BYTES - 2 * (sum(t.shape[1] for t in (train_query, train_key, train_value)) * full)
     grant -= 2 * seats * norm_length
     vmem = pl.BlockSpec(memory_space=pltpu.VMEM)
@@ -278,12 +315,12 @@
         out_specs=[vmem] * 4,
         scratch_shapes=[pltpu.VMEM(a.shape, a.dtype) for a in args]
         + [
-            pltpu.VMEM((seats, 1, norm_length), jnp.float32),
+            pltpu.VMEM((size, tp_size, 1, norm_length), jnp.float32),
             pltpu.SemaphoreType.DMA((11,)),
-            pltpu.SemaphoreType.DMA((3, size, count)),
-            pltpu.SemaphoreType.DMA((size, count)),
-            pltpu.SemaphoreType.DMA((seats,)),
-            pltpu.SemaphoreType.DMA((seats,)),
+            pltpu.SemaphoreType.DMA((3, size, count + 1)),
+            pltpu.SemaphoreType.DMA((size, count + 1)),
+            pltpu.SemaphoreType.DMA((tp_size,)),
+            pltpu.SemaphoreType.DMA((tp_size,)),
         ],
         compiler_params=pltpu.CompilerParams(
             collective_id=0, has_side_effects=True, vmem_limit_bytes=grant
@@ -350,7 +387,7 @@
         fits = (
             size % 2 == 0
             and size >= 4
-            and all(t.shape[0] % 128 == 0 and t.shape[1] % CHUNK_ROWS == 0 for t in trains)
+            and all(t.shape[0] % 128 == 0 and t.shape[1] % FIRST_ROWS == 0 for t in trains)
             and args[9].shape[0] % 128 == 0
         )
         return fused(size, tp_size, *args) if fits else plain(*args)

time: 72.6 us -> 70 us (0.964)
  Pallas kernels: 71.8 us -> 69.2 us
    pallas_call x1, Pallas kernels: 69.1 us -> 66.5 us  [fused(): pl.pallas_call(functools.partial(kernel, size, tp_size), out_shape=outs,...]
where the time goes in v3:
time: 70 us; the launch traced here: 69.8 us
  Pallas kernels  69.2 us (99%)
    pallas_call x1, Pallas kernels, fused(): pl.pallas_call(functools.partial(kernel, size, tp_size), out_shape=outs,...  66.5 us
    pallas_call x1, Pallas kernels, store_out(): pl.pallas_call(store_kernel, out_shape=[jax.ShapeDtypeStruct(a.shape, a.d...  2.71 us

profile of v3, /device:TPU:0, one launch (start us, length us, event | category | flops | bytes accessed | tf_op | source)
XLA Modules:
  0.0 69.8 jit_solution(11022188700209379372)
XLA Ops:
  0.6 66.5 %shard_map.138 = (bf16[1024,2048]{1,0:T(8,128)(2,1)S(1)}, bf16[256,2048]{1,0:T(8,128)(2,1)S(1)}, bf16[256,2048]{1,0:T(8,128)(2,1)S(1)}, bf16[16,128]{1,0:T(8,128)(2,1)S(1)}) custom-call(bf16[256,1024]{1,0:T(8,128)(2,1)} %refs_0_.1, bf16[16,256]{1,0:T(8,128)(2,1)} %bitcast.6, bf16[16,1024]{1,0:T(8,128)(2,1)} %refs_2_.1, bf16[256,256]{1,0:T(8,128)(2,1)} %refs_3_.1, ...), custom_call_target="tpu_custom_call" | custom-call | tf_op jit(solution)/shard_map/pallas_call | solution.py:311
  67.1 2.7 %shard_map.139 = (bf16[1024,2048]{1,0:T(8,128)(2,1)}, bf16[256,2048]{1,0:T(8,128)(2,1)}, bf16[256,2048]{1,0:T(8,128)(2,1)}, bf16[16,128]{1,0:T(8,128)(2,1)}) custom-call(bf16[1024,2048]{1,0:T(8,128)(2,1)S(1)} %get-tuple-element.12.refs_0_, bf16[256,2048]{1,0:T(8,128)(2,1)S(1)} %get-tuple-element.13.refs_1_, bf16[256,2048]{1,0:T(8,128)(2,1)S(1)} %get-tuple-element.14.refs_2_, ...), custom_call_target="tpu_custom_call" | custom-call | tf_op jit(solution)/shard_map/pallas_call | solution.py:343
